TPU v7x, 512 devices: a whole 4x4x16 slice. The times are simulated.
512 devices in a mesh: rows: 128 (over x, z_lo, y), cols: 4 (over z_hi, core).
Axes of the slice: x: 4, y: 4, z: 16 (z_hi: 2, z_lo: 8; z = z_hi * 8 + z_lo), core: 2. Of those that a mesh axis runs over, the one named last changes fastest.
Arguments:
- coords: int32 [8, 262144], P(None, ('rows', 'cols')), may hold values from 0 to 4095
- probes: float32 [64, 262144], P(None, ('rows', 'cols')), may hold values from -6 to 6
- lengthscales: float32 [8], replicated, may hold values from 0.15 to 0.25
- amplitude: float32 [1], replicated, may hold values from 0.1 to 0.3
- landmarks: float32 [254, 8, 128], replicated, may hold values from 0 to 1
- coupling: float32 [128, 128], replicated, may hold values from -0.5 to 0.5
Outputs:
- products: float32 [2, 64, 262144], P(None, None, ('rows', 'cols'))
All inputs are finite; a program needn't handle non-finite values.
Results may differ from a plain program's by a relative error of at most 0.0025.
Values may be sent and summed in bfloat16 or wider, within the bound.
No kernel may reach another device: no remote copies, remote signals or barrier semaphores. Data moves between devices by JAX's collectives and lax.ppermute only.
A program may use at most 64 MiB of HBM per device.

v0:
```python
import jax
import jax.numpy as jnp
from jax import lax
from jax.sharding import PartitionSpec as P


def over_pieces(array, axis):
    return lax.all_gather(array, axis).sum(0)


def swapped(array, axis, apart):
    return lax.ppermute(array, axis, [(i, i ^ 1 << apart) for i in range(lax.axis_size(axis))])


def pair_squares(left_points, right_points):
    squared = jnp.zeros((left_points.shape[1], right_points.shape[1]), jnp.float32)
    for component in range(left_points.shape[0]):
        offset = left_points[component][:, None] - right_points[component][None, :]
        squared = squared + offset * offset
    return squared


def on_device(coords, probes, lengthscales, amplitude, landmarks, coupling):
    highest = lax.Precision.HIGHEST
    inverse_scale = 1.0 / lengthscales
    scaled = coords.astype(jnp.float32) * (1.0 / 4096.0) * inverse_scale[:, None]
    strength = amplitude[0]
    signs_half = probes.astype(jnp.bfloat16)
    width = coords.shape[1]
    groups = lax.axis_size("cols")
    rows_index = lax.axis_index("rows")
    levels = lax.axis_size("rows").bit_length() - 1
    leaf_points = lax.all_gather(scaled, "cols", axis=1, tiled=True)
    leaf_signs = lax.all_gather(signs_half, "cols", axis=1, tiled=True)
    accumulated = jnp.zeros((2, probes.shape[0], width), jnp.float32)
    for row_block in range(groups):
        block_points = leaf_points[:, row_block * width : (row_block + 1) * width]
        block_signs = leaf_signs[:, row_block * width : (row_block + 1) * width]
        squared = pair_squares(block_points, scaled)
        kernel = strength * jnp.exp(-0.5 * squared)
        kernel_half = kernel.astype(jnp.bfloat16)
        slope_half = (kernel * squared).astype(jnp.bfloat16)
        accumulated = accumulated + jnp.stack(
            [
                jnp.dot(block_signs, kernel_half, preferred_element_type=jnp.float32),
                jnp.dot(block_signs, slope_half, preferred_element_type=jnp.float32),
            ]
        )
    result = accumulated
    factor_list = []
    dfactor_list = []
    for level in range(levels):
        depth = levels - level
        node = jnp.right_shift(rows_index, level)
        chosen = lax.dynamic_index_in_dim(landmarks, 2**depth - 2 + node, 0, keepdims=False)
        squared = pair_squares(scaled, chosen * inverse_scale[:, None])
        factor = strength * jnp.exp(-0.5 * squared)
        factor_list.append(factor)
        dfactor_list.append(factor * squared)
    factor_stack = jnp.stack(factor_list)
    dfactor_stack = jnp.stack(dfactor_list)
    own_project = jnp.einsum("pn,lnr->lpr", probes, factor_stack, precision=highest)
    own_dproject = jnp.einsum("pn,lnr->lpr", probes, dfactor_stack, precision=highest)
    projections = over_pieces(jnp.stack([own_project, own_dproject], axis=1), "cols")
    siblings = []
    pending = projections
    for level in range(levels):
        partner = swapped(pending[level:], "rows", level)
        siblings.append(partner[0])
        pending = pending.at[level + 1 :].add(partner[1:])
    for level in range(levels):
        sibling_sums = siblings[level]
        is_left = jnp.right_shift(rows_index, level) & 1 == 0
        core = jnp.where(is_left, coupling.T, coupling)
        first = jnp.dot(sibling_sums[0], core, precision=highest)
        second = jnp.dot(sibling_sums[1], core, precision=highest)
        value = jnp.dot(first, factor_stack[level].T, precision=highest)
        slope = jnp.dot(first, dfactor_stack[level].T, precision=highest) + jnp.dot(
            second, factor_stack[level].T, precision=highest
        )
        result = result + jnp.stack([value, slope])
    return result


def solution(mesh):
    in_specs = (P(None, ("rows", "cols")), P(None, ("rows", "cols")), P(), P(), P(), P())
    out_specs = P(None, None, ("rows", "cols"))
    return jax.shard_map(
        on_device, mesh=mesh, in_specs=in_specs, out_specs=out_specs, check_vma=False
    )
```

profile of v0, /device:TPU:8, one launch (start us, length us, event | category | flops | bytes accessed | tf_op | source)
XLA Modules:
  0.0 196.0 jit_solution(11825295575556073980)
XLA Ops:
  14.0 1.2 convolution_bitcast_fusion
  15.2 1.2 convolution_bitcast_fusion.1
  17.2 17.0 %all_gather.12 = f32[8,2048]{1,0:T(8,128)S(1)} all-gather(f32[8,512]{1,0:T(8,128)S(1)} %convert_multiply_fusion), channel_id=1, replica_groups=mesh['rows'=128,'cols'=4] {'cols'}, dimensions={1}, use_global_device_ids=true | all-gather | bytes 81920 | tf_op jit(solution)/shard_map/all_gather | solution.py:33
  34.3 18.0 %all_gather.13 = bf16[64,2048]{1,0:T(8,128)(2,1)S(1)} all-gather(bf16[64,512]{1,0:T(8,128)(2,1)S(1)} %convert_element_type.32), channel_id=1, replica_groups=mesh['rows'=128,'cols'=4] {'cols'}, dimensions={1}, use_global_device_ids=true | all-gather | bytes 327680 | tf_op jit(solution)/shard_map/all_gather | solution.py:34
  52.3 1.1 convolution_bitcast_fusion.3
  53.4 1.2 convolution_bitcast_fusion.2
  54.7 1.1 convolution_bitcast_fusion.5
  55.8 1.2 convolution_bitcast_fusion.4
  57.0 1.1 convolution_bitcast_fusion.7
  58.2 1.2 convolution_bitcast_fusion.6
  59.4 11.6 %all-gather.3.cloned.1.call-done = f32[28,2,64,128]{3,2,0,1:T(8,128)} async-done(((f32[7,2,64,128]{3,2,0,1:T(8,128)}), f32[28,2,64,128]{3,2,0,1:T(8,128)}) %all-gather.3.cloned.1.call-update) | async-done | bytes 1835024 | tf_op jit(solution)/shard_map/all_gather | solution.py:8
  71.1 1.7 reduce_sum.9
  72.7 3.6 %collective-permute-start = (f32[7,2,64,128]{3,2,0,1:T(8,128)S(1)}, f32[7,2,64,128]{3,2,0,1:T(8,128)S(1)}, u32[]{:S(2)}, u32[]{:S(2)}) collective-permute-start(f32[7,2,64,128]{3,2,0,1:T(8,128)S(1)} %reduce_sum.9), channel_id=1, source_target_pairs={{0,4},{4,0},{8,12},{12,8},{16,20},{20,16},{24,28},{28,24},{32,36},... | collective-permute-start | bytes 1376264 | tf_op jit(solution)/shard_map/ppermute | solution.py:12
  76.3 1.1 convolution_bitcast_fusion.9
  77.6 1.2 convolution_bitcast_fusion.8
  78.9 8.4 %collective-permute-done = f32[7,2,64,128]{3,2,0,1:T(8,128)S(1)} collective-permute-done((f32[7,2,64,128]{3,2,0,1:T(8,128)S(1)}, f32[7,2,64,128]{3,2,0,1:T(8,128)S(1)}, u32[]{:S(2)}, u32[]{:S(2)}) %collective-permute-start) | collective-permute-done | bytes 458784 | tf_op jit(solution)/shard_map/ppermute | solution.py:12
  87.3 4.4 %collective-permute-start.1 = (f32[6,2,64,128]{3,2,0,1:T(8,128)S(1)}, f32[6,2,64,128]{3,2,0,1:T(8,128)S(1)}, u32[]{:S(2)}, u32[]{:S(2)}) collective-permute-start(f32[6,2,64,128]{3,2,0,1:T(8,128)S(1)} %slice_add_fusion), channel_id=1, source_target_pairs={{0,8},{4,12},{8,0},{12,4},{16,24},{20,28},{24,16},{28,20},{32,40},... | collective-permute-start | bytes 1179656 | tf_op jit(solution)/shard_map/ppermute | solution.py:12
  92.0 1.0 convolution_bitcast_fusion.16
  93.2 1.0 fusion.52
  94.1 1.0 fusion.6
  95.1 6.0 %collective-permute-done.1 = f32[6,2,64,128]{3,2,0,1:T(8,128)S(1)} collective-permute-done((f32[6,2,64,128]{3,2,0,1:T(8,128)S(1)}, f32[6,2,64,128]{3,2,0,1:T(8,128)S(1)}, u32[]{:S(2)}, u32[]{:S(2)}) %collective-permute-start.1) | collective-permute-done | bytes 393248 | tf_op jit(solution)/shard_map/ppermute | solution.py:12
  101.2 7.4 %collective-permute-start.2 = (f32[5,2,64,128]{3,2,0,1:T(8,128)S(1)}, f32[5,2,64,128]{3,2,0,1:T(8,128)S(1)}, u32[]{:S(2)}, u32[]{:S(2)}) collective-permute-start(f32[5,2,64,128]{3,2,0,1:T(8,128)S(1)} %slice_add_fusion.1), channel_id=1, source_target_pairs={{0,16},{4,20},{8,24},{12,28},{16,0},{20,4},{24,8},{28,12},{32,48},... | collective-permute-start | bytes 983048 | tf_op jit(solution)/shard_map/ppermute | solution.py:12
  109.0 1.0 fusion.50
  110.0 1.0 convolution_bitcast_fusion.15
  111.0 1.0 fusion.5
  112.0 3.0 %collective-permute-done.2 = f32[5,2,64,128]{3,2,0,1:T(8,128)S(1)} collective-permute-done((f32[5,2,64,128]{3,2,0,1:T(8,128)S(1)}, f32[5,2,64,128]{3,2,0,1:T(8,128)S(1)}, u32[]{:S(2)}, u32[]{:S(2)}) %collective-permute-start.2) | collective-permute-done | bytes 327712 | tf_op jit(solution)/shard_map/ppermute | solution.py:12
  115.0 7.8 %collective-permute-start.3 = (f32[4,2,64,128]{3,2,0,1:T(8,128)S(1)}, f32[4,2,64,128]{3,2,0,1:T(8,128)S(1)}, u32[]{:S(2)}, u32[]{:S(2)}) collective-permute-start(f32[4,2,64,128]{3,2,0,1:T(8,128)S(1)} %slice_add_fusion.2), channel_id=1, source_target_pairs={{0,32},{4,36},{8,40},{12,44},{16,48},{20,52},{24,56},{28,60},{32,0... | collective-permute-start | bytes 786440 | tf_op jit(solution)/shard_map/ppermute | solution.py:12
  123.0 1.0 fusion.48
  124.2 1.0 convolution_bitcast_fusion.14
  125.2 1.0 fusion.4
  126.2 6.7 %collective-permute-done.3 = f32[4,2,64,128]{3,2,0,1:T(8,128)S(1)} collective-permute-done((f32[4,2,64,128]{3,2,0,1:T(8,128)S(1)}, f32[4,2,64,128]{3,2,0,1:T(8,128)S(1)}, u32[]{:S(2)}, u32[]{:S(2)}) %collective-permute-start.3) | collective-permute-done | bytes 262176 | tf_op jit(solution)/shard_map/ppermute | solution.py:12
  132.8 21.1 %collective-permute-start.4 = (f32[3,2,64,128]{3,2,0,1:T(8,128)S(1)}, f32[3,2,64,128]{3,2,0,1:T(8,128)S(1)}, u32[]{:S(2)}, u32[]{:S(2)}) collective-permute-start(f32[3,2,64,128]{3,2,0,1:T(8,128)S(1)} %slice_add_fusion.3), channel_id=1, source_target_pairs={{0,64},{4,68},{8,72},{12,76},{16,80},{20,84},{24,88},{28,92},{32,9... | collective-permute-start | bytes 589832 | tf_op jit(solution)/shard_map/ppermute | solution.py:12
  154.2 1.0 fusion.46
  155.4 1.0 convolution_bitcast_fusion.13
  156.4 1.0 fusion.3
  157.3 11.9 %collective-permute-done.4 = f32[3,2,64,128]{3,2,0,1:T(8,128)S(1)} collective-permute-done((f32[3,2,64,128]{3,2,0,1:T(8,128)S(1)}, f32[3,2,64,128]{3,2,0,1:T(8,128)S(1)}, u32[]{:S(2)}, u32[]{:S(2)}) %collective-permute-start.4) | collective-permute-done | bytes 196640 | tf_op jit(solution)/shard_map/ppermute | solution.py:12
  169.2 3.6 %collective-permute-start.5 = (f32[2,2,64,128]{3,2,0,1:T(8,128)S(1)}, f32[2,2,64,128]{3,2,0,1:T(8,128)S(1)}, u32[]{:S(2)}, u32[]{:S(2)}) collective-permute-start(f32[2,2,64,128]{3,2,0,1:T(8,128)S(1)} %slice_add_fusion.4), channel_id=1, source_target_pairs={{0,128},{4,132},{8,136},{12,140},{16,144},{20,148},{24,152},{28,15... | collective-permute-start | bytes 393224 | tf_op jit(solution)/shard_map/ppermute | solution.py:12
  173.1 1.0 fusion.44
  174.3 1.0 fusion.2
  175.2 1.0 convolution_bitcast_fusion.12
  176.6 4.9 %collective-permute-start.6 = (f32[1,2,64,128]{3,2,0,1:T(8,128)S(1)}, f32[1,2,64,128]{3,2,0,1:T(8,128)S(1)}, u32[]{:S(2)}, u32[]{:S(2)}) collective-permute-start(f32[1,2,64,128]{3,2,0,1:T(8,128)S(1)} %slice_add_fusion.5), channel_id=1, source_target_pairs={{0,256},{4,260},{8,264},{12,268},{16,272},{20,276},{24,280},{28,28... | collective-permute-start | bytes 196616 | tf_op jit(solution)/shard_map/ppermute | solution.py:12
  181.7 1.0 fusion.42
  182.8 1.0 fusion.1
  183.8 1.0 convolution_bitcast_fusion.11
  185.0 1.0 convolution_bitcast_fusion.10
  186.0 1.0 fusion.40
  187.2 1.0 fusion
  188.2 1.0 fusion.39
  (48 shorter events, 10.8 us)
Async XLA Ops:
  6.5 64.5 %all-gather.3.cloned.1.call-start = ((), (), s32[]{:S(2)}) async-start(), calls=%async_computation | async-start | bytes 2293760 | tf_op jit(solution)/shard_map/all_gather | solution.py:8
  10.2 3.8 %copy-start.1 = (f32[64,512]{1,0:T(8,128)S(1)}, f32[64,512]{1,0:T(8,128)}, u32[]{:S(2)}) copy-start(f32[64,512]{1,0:T(8,128)} %param.19) | copy-start | bytes 393220
  72.7 14.5 %collective-permute-start = (f32[7,2,64,128]{3,2,0,1:T(8,128)S(1)}, f32[7,2,64,128]{3,2,0,1:T(8,128)S(1)}, u32[]{:S(2)}, u32[]{:S(2)}) collective-permute-start(f32[7,2,64,128]{3,2,0,1:T(8,128)S(1)} %reduce_sum.9), channel_id=1, source_target_pairs={{0,4},{4,0},{8,12},{12,8},{16,20},{20,16},{24,28},{28,24},{32,36},... | collective-permute-start | bytes 1376264 | tf_op jit(solution)/shard_map/ppermute | solution.py:12
  76.3 1.2 copy-start
  87.3 13.8 %collective-permute-start.1 = (f32[6,2,64,128]{3,2,0,1:T(8,128)S(1)}, f32[6,2,64,128]{3,2,0,1:T(8,128)S(1)}, u32[]{:S(2)}, u32[]{:S(2)}) collective-permute-start(f32[6,2,64,128]{3,2,0,1:T(8,128)S(1)} %slice_add_fusion), channel_id=1, source_target_pairs={{0,8},{4,12},{8,0},{12,4},{16,24},{20,28},{24,16},{28,20},{32,40},... | collective-permute-start | bytes 1179656 | tf_op jit(solution)/shard_map/ppermute | solution.py:12
  101.2 13.8 %collective-permute-start.2 = (f32[5,2,64,128]{3,2,0,1:T(8,128)S(1)}, f32[5,2,64,128]{3,2,0,1:T(8,128)S(1)}, u32[]{:S(2)}, u32[]{:S(2)}) collective-permute-start(f32[5,2,64,128]{3,2,0,1:T(8,128)S(1)} %slice_add_fusion.1), channel_id=1, source_target_pairs={{0,16},{4,20},{8,24},{12,28},{16,0},{20,4},{24,8},{28,12},{32,48},... | collective-permute-start | bytes 983048 | tf_op jit(solution)/shard_map/ppermute | solution.py:12
  115.0 17.8 %collective-permute-start.3 = (f32[4,2,64,128]{3,2,0,1:T(8,128)S(1)}, f32[4,2,64,128]{3,2,0,1:T(8,128)S(1)}, u32[]{:S(2)}, u32[]{:S(2)}) collective-permute-start(f32[4,2,64,128]{3,2,0,1:T(8,128)S(1)} %slice_add_fusion.2), channel_id=1, source_target_pairs={{0,32},{4,36},{8,40},{12,44},{16,48},{20,52},{24,56},{28,60},{32,0... | collective-permute-start | bytes 786440 | tf_op jit(solution)/shard_map/ppermute | solution.py:12
  132.8 36.4 %collective-permute-start.4 = (f32[3,2,64,128]{3,2,0,1:T(8,128)S(1)}, f32[3,2,64,128]{3,2,0,1:T(8,128)S(1)}, u32[]{:S(2)}, u32[]{:S(2)}) collective-permute-start(f32[3,2,64,128]{3,2,0,1:T(8,128)S(1)} %slice_add_fusion.3), channel_id=1, source_target_pairs={{0,64},{4,68},{8,72},{12,76},{16,80},{20,84},{24,88},{28,92},{32,9... | collective-permute-start | bytes 589832 | tf_op jit(solution)/shard_map/ppermute | solution.py:12
  169.2 7.3 %collective-permute-start.5 = (f32[2,2,64,128]{3,2,0,1:T(8,128)S(1)}, f32[2,2,64,128]{3,2,0,1:T(8,128)S(1)}, u32[]{:S(2)}, u32[]{:S(2)}) collective-permute-start(f32[2,2,64,128]{3,2,0,1:T(8,128)S(1)} %slice_add_fusion.4), channel_id=1, source_target_pairs={{0,128},{4,132},{8,136},{12,140},{16,144},{20,148},{24,152},{28,15... | collective-permute-start | bytes 393224 | tf_op jit(solution)/shard_map/ppermute | solution.py:12
  176.6 8.2 %collective-permute-start.6 = (f32[1,2,64,128]{3,2,0,1:T(8,128)S(1)}, f32[1,2,64,128]{3,2,0,1:T(8,128)S(1)}, u32[]{:S(2)}, u32[]{:S(2)}) collective-permute-start(f32[1,2,64,128]{3,2,0,1:T(8,128)S(1)} %slice_add_fusion.5), channel_id=1, source_target_pairs={{0,256},{4,260},{8,264},{12,268},{16,272},{20,276},{24,280},{28,28... | collective-permute-start | bytes 196616 | tf_op jit(solution)/shard_map/ppermute | solution.py:12
Sparse Core Ops, SparseCore 0:
  17.3 53.6 all-gather.2
where the time goes:
time: 197 us; the launch traced here: 196 us
  starting transfers between devices  52.9 us (27%)
  waiting for transfers between devices  48 us (24%)
  matrix products  35.1 us (18%)
  blocking collectives  35 us (18%)
  between operations  14.5 us (7%)
  other arithmetic  10.3 us (5%)
    ppermute x7, starting transfers between devices, swapped(): lax.ppermute(array, axis, [(i, i ^ 1 << apart) for i in range(lax.axis_si...  52.9 us
    ppermute x7, waiting for transfers between devices, swapped(): lax.ppermute(array, axis, [(i, i ^ 1 << apart) for i in range(lax.axis_si...  36.3 us
    all_gather x1, blocking collectives, on_device(): leaf_signs = lax.all_gather(signs_half, 'cols', axis=1, tiled=True)  18 us
    all_gather x1, blocking collectives, on_device(): leaf_points = lax.all_gather(scaled, 'cols', axis=1, tiled=True)  17 us
    all_gather x1, waiting for transfers between devices, over_pieces(): return lax.all_gather(array, axis).sum(0)  11.6 us
    dot_general x7, matrix products, on_device(): jnp.dot(first, dfactor_stack[level].T, precision=highest)  6.9 us
    dot_general x7, matrix products, on_device(): jnp.dot(second, factor_stack[level].T, precision=highest)  6.89 us
    dot_general x7, matrix products, on_device(): value = jnp.dot(first, factor_stack[level].T, precision=highest)  6.88 us
  transfers between devices with their start and end apart: 8, of which 7 were waited for; matrix products, arithmetic and copies ran while one was open for 15% of the time, Pallas kernels for 0%

commit v1 on v0

--- a/solution.py
+++ b/solution.py
@@ -31,7 +31,9 @@
     rows_index = lax.axis_index("rows")
     levels = lax.axis_size("rows").bit_length() - 1
     leaf_points = lax.all_gather(scaled, "cols", axis=1, tiled=True)
-    leaf_signs = lax.all_gather(signs_half, "cols", axis=1, tiled=True)
+    leaf_signs = jnp.concatenate(
+        lax.all_to_all(jnp.stack([signs_half] * lax.axis_size("cols")), "cols", 0, 0), axis=1
+    )
     accumulated = jnp.zeros((2, probes.shape[0], width), jnp.float32)
     for row_block in range(groups):
         block_points = leaf_points[:, row_block * width : (row_block + 1) * width]

time: 197 us -> 203 us (1.030)
  the two profiles are of different devices: /device:TPU:8 before, /device:TPU:1 now
where the time goes in v1:
time: 203 us
  waiting for transfers between devices  79.1 us (39%)
  starting transfers between devices  44.4 us (22%)
  matrix products  35.1 us (17%)
  blocking collectives  18.5 us (9%)
  between operations  14.5 us (7%)
  other arithmetic  10.4 us (5%)
    ppermute x7, waiting for transfers between devices, swapped(): lax.ppermute(array, axis, [(i, i ^ 1 << apart) for i in range(lax.axis_si...  43.6 us
    all_gather x1, waiting for transfers between devices, over_pieces(): return lax.all_gather(array, axis).sum(0)  35.5 us
    ppermute x7, starting transfers between devices, swapped(): lax.ppermute(array, axis, [(i, i ^ 1 << apart) for i in range(lax.axis_si...  27.8 us
    all_gather x1, blocking collectives, on_device(): leaf_points = lax.all_gather(scaled, 'cols', axis=1, tiled=True)  18.5 us
    all_to_all x1, starting transfers between devices, on_device(): lax.all_to_all(jnp.stack([signs_half] * lax.axis_size('cols')), 'cols', 0...  16.6 us
    dot_general x7, matrix products, on_device(): jnp.dot(first, dfactor_stack[level].T, precision=highest)  6.9 us
    dot_general x7, matrix products, on_device(): jnp.dot(second, factor_stack[level].T, precision=highest)  6.89 us
    dot_general x7, matrix products, on_device(): value = jnp.dot(first, factor_stack[level].T, precision=highest)  6.88 us
  transfers between devices with their start and end apart: 9, of which 6 were waited for; matrix products, arithmetic and copies ran while one was open for 15% of the time, Pallas kernels for 0%

profile of v1, /device:TPU:1, one launch (start us, length us, event | category | flops | bytes accessed | tf_op | source)
XLA Modules:
  0.0 202.9 jit_solution(12443829410471080058)
XLA Ops:
  14.0 1.2 convolution_bitcast_fusion
  15.2 1.2 convolution_bitcast_fusion.1
  18.0 16.6 %all-to-all-start = ((bf16[4,64,512]{2,1,0:T(8,128)(2,1)}), bf16[4,64,512]{2,1,0:T(8,128)(2,1)S(1)}, u32[]{:S(2)}, u32[]{:S(2)}) async-start(bf16[4,64,512]{2,1,0:T(8,128)(2,1)} %stack.135), calls=%async_computation | async-start | bytes 524288 | tf_op jit(solution)/shard_map/all_to_all | solution.py:35
  34.7 18.5 %all_gather.9 = f32[8,2048]{1,0:T(8,128)S(1)} all-gather(f32[8,512]{1,0:T(8,128)S(1)} %convert_multiply_fusion), channel_id=1, replica_groups=mesh['rows'=128,'cols'=4] {'cols'}, dimensions={1}, use_global_device_ids=true | all-gather | bytes 81920 | tf_op jit(solution)/shard_map/all_gather | solution.py:33
  53.3 1.1 convolution_bitcast_fusion.3
  54.5 1.2 convolution_bitcast_fusion.2
  55.7 1.1 convolution_bitcast_fusion.5
  56.8 1.2 convolution_bitcast_fusion.4
  58.1 1.1 convolution_bitcast_fusion.7
  59.2 1.2 convolution_bitcast_fusion.6
  60.4 35.5 %all-gather.3.cloned.1.call-done = f32[28,2,64,128]{3,2,0,1:T(8,128)} async-done(((f32[7,2,64,128]{3,2,0,1:T(8,128)}), f32[28,2,64,128]{3,2,0,1:T(8,128)}) %all-gather.3.cloned.1.call-update) | async-done | bytes 1835024 | tf_op jit(solution)/shard_map/all_gather | solution.py:8
  95.9 1.7 reduce_sum.9
  97.6 1.9 collective-permute-start
  99.5 1.1 convolution_bitcast_fusion.9
  100.7 1.2 convolution_bitcast_fusion.8
  101.9 9.4 %collective-permute-done = f32[7,2,64,128]{3,2,0,1:T(8,128)S(1)} collective-permute-done((f32[7,2,64,128]{3,2,0,1:T(8,128)S(1)}, f32[7,2,64,128]{3,2,0,1:T(8,128)S(1)}, u32[]{:S(2)}, u32[]{:S(2)}) %collective-permute-start) | collective-permute-done | bytes 458784 | tf_op jit(solution)/shard_map/ppermute | solution.py:12
  111.3 5.0 %collective-permute-start.1 = (f32[6,2,64,128]{3,2,0,1:T(8,128)S(1)}, f32[6,2,64,128]{3,2,0,1:T(8,128)S(1)}, u32[]{:S(2)}, u32[]{:S(2)}) collective-permute-start(f32[6,2,64,128]{3,2,0,1:T(8,128)S(1)} %slice_add_fusion), channel_id=1, source_target_pairs={{0,8},{4,12},{8,0},{12,4},{16,24},{20,28},{24,16},{28,20},{32,40},... | collective-permute-start | bytes 1179656 | tf_op jit(solution)/shard_map/ppermute | solution.py:12
  116.6 1.0 convolution_bitcast_fusion.16
  117.8 1.0 fusion.52
  118.7 1.0 fusion.6
  119.7 4.5 %collective-permute-done.1 = f32[6,2,64,128]{3,2,0,1:T(8,128)S(1)} collective-permute-done((f32[6,2,64,128]{3,2,0,1:T(8,128)S(1)}, f32[6,2,64,128]{3,2,0,1:T(8,128)S(1)}, u32[]{:S(2)}, u32[]{:S(2)}) %collective-permute-start.1) | collective-permute-done | bytes 393248 | tf_op jit(solution)/shard_map/ppermute | solution.py:12
  124.3 6.3 %collective-permute-start.2 = (f32[5,2,64,128]{3,2,0,1:T(8,128)S(1)}, f32[5,2,64,128]{3,2,0,1:T(8,128)S(1)}, u32[]{:S(2)}, u32[]{:S(2)}) collective-permute-start(f32[5,2,64,128]{3,2,0,1:T(8,128)S(1)} %slice_add_fusion.1), channel_id=1, source_target_pairs={{0,16},{4,20},{8,24},{12,28},{16,0},{20,4},{24,8},{28,12},{32,48},... | collective-permute-start | bytes 983048 | tf_op jit(solution)/shard_map/ppermute | solution.py:12
  131.0 1.0 fusion.50
  132.0 1.0 convolution_bitcast_fusion.15
  133.0 1.0 fusion.5
  134.0 3.0 %collective-permute-done.2 = f32[5,2,64,128]{3,2,0,1:T(8,128)S(1)} collective-permute-done((f32[5,2,64,128]{3,2,0,1:T(8,128)S(1)}, f32[5,2,64,128]{3,2,0,1:T(8,128)S(1)}, u32[]{:S(2)}, u32[]{:S(2)}) %collective-permute-start.2) | collective-permute-done | bytes 327712 | tf_op jit(solution)/shard_map/ppermute | solution.py:12
  137.0 2.7 %collective-permute-start.3 = (f32[4,2,64,128]{3,2,0,1:T(8,128)S(1)}, f32[4,2,64,128]{3,2,0,1:T(8,128)S(1)}, u32[]{:S(2)}, u32[]{:S(2)}) collective-permute-start(f32[4,2,64,128]{3,2,0,1:T(8,128)S(1)} %slice_add_fusion.2), channel_id=1, source_target_pairs={{0,32},{4,36},{8,40},{12,44},{16,48},{20,52},{24,56},{28,60},{32,0... | collective-permute-start | bytes 786440 | tf_op jit(solution)/shard_map/ppermute | solution.py:12
  139.9 1.0 fusion.48
  141.0 1.0 convolution_bitcast_fusion.14
  142.0 1.0 fusion.4
  143.0 9.7 %collective-permute-done.3 = f32[4,2,64,128]{3,2,0,1:T(8,128)S(1)} collective-permute-done((f32[4,2,64,128]{3,2,0,1:T(8,128)S(1)}, f32[4,2,64,128]{3,2,0,1:T(8,128)S(1)}, u32[]{:S(2)}, u32[]{:S(2)}) %collective-permute-start.3) | collective-permute-done | bytes 262176 | tf_op jit(solution)/shard_map/ppermute | solution.py:12
  152.8 4.0 %collective-permute-start.4 = (f32[3,2,64,128]{3,2,0,1:T(8,128)S(1)}, f32[3,2,64,128]{3,2,0,1:T(8,128)S(1)}, u32[]{:S(2)}, u32[]{:S(2)}) collective-permute-start(f32[3,2,64,128]{3,2,0,1:T(8,128)S(1)} %slice_add_fusion.3), channel_id=1, source_target_pairs={{0,64},{4,68},{8,72},{12,76},{16,80},{20,84},{24,88},{28,92},{32,9... | collective-permute-start | bytes 589832 | tf_op jit(solution)/shard_map/ppermute | solution.py:12
  156.9 1.0 fusion.46
  158.1 1.0 convolution_bitcast_fusion.13
  159.1 1.0 fusion.3
  160.1 16.9 %collective-permute-done.4 = f32[3,2,64,128]{3,2,0,1:T(8,128)S(1)} collective-permute-done((f32[3,2,64,128]{3,2,0,1:T(8,128)S(1)}, f32[3,2,64,128]{3,2,0,1:T(8,128)S(1)}, u32[]{:S(2)}, u32[]{:S(2)}) %collective-permute-start.4) | collective-permute-done | bytes 196640 | tf_op jit(solution)/shard_map/ppermute | solution.py:12
  177.0 3.5 %collective-permute-start.5 = (f32[2,2,64,128]{3,2,0,1:T(8,128)S(1)}, f32[2,2,64,128]{3,2,0,1:T(8,128)S(1)}, u32[]{:S(2)}, u32[]{:S(2)}) collective-permute-start(f32[2,2,64,128]{3,2,0,1:T(8,128)S(1)} %slice_add_fusion.4), channel_id=1, source_target_pairs={{0,128},{4,132},{8,136},{12,140},{16,144},{20,148},{24,152},{28,15... | collective-permute-start | bytes 393224 | tf_op jit(solution)/shard_map/ppermute | solution.py:12
  180.7 1.0 fusion.44
  181.9 1.0 fusion.2
  182.9 1.0 convolution_bitcast_fusion.12
  183.9 4.4 %collective-permute-start.6 = (f32[1,2,64,128]{3,2,0,1:T(8,128)S(1)}, f32[1,2,64,128]{3,2,0,1:T(8,128)S(1)}, u32[]{:S(2)}, u32[]{:S(2)}) collective-permute-start(f32[1,2,64,128]{3,2,0,1:T(8,128)S(1)} %slice_add_fusion.5), channel_id=1, source_target_pairs={{0,256},{4,260},{8,264},{12,268},{16,272},{20,276},{24,280},{28,28... | collective-permute-start | bytes 196616 | tf_op jit(solution)/shard_map/ppermute | solution.py:12
  188.5 1.0 fusion.42
  189.7 1.0 fusion.1
  190.7 1.0 convolution_bitcast_fusion.11
  191.9 1.0 convolution_bitcast_fusion.10
  192.9 1.0 fusion.40
  194.0 1.0 fusion
  195.0 1.0 fusion.39
  (51 shorter events, 11.3 us)
Async XLA Ops:
  6.5 89.4 %all-gather.3.cloned.1.call-start = ((), (), s32[]{:S(2)}) async-start(), calls=%async_computation.1 | async-start | bytes 2293760 | tf_op jit(solution)/shard_map/all_gather | solution.py:8
  10.2 3.8 %copy-start.1 = (f32[64,512]{1,0:T(8,128)S(1)}, f32[64,512]{1,0:T(8,128)}, u32[]{:S(2)}) copy-start(f32[64,512]{1,0:T(8,128)} %param.19) | copy-start | bytes 393220
  15.2 19.3 %copy-start = (f32[128,128]{1,0:T(8,128)S(1)}, f32[128,128]{1,0:T(8,128)}, u32[]{:S(2)}) copy-start(f32[128,128]{1,0:T(8,128)} %param.23) | copy-start | bytes 196612
  18.0 35.3 %all-to-all-start = ((bf16[4,64,512]{2,1,0:T(8,128)(2,1)}), bf16[4,64,512]{2,1,0:T(8,128)(2,1)S(1)}, u32[]{:S(2)}, u32[]{:S(2)}) async-start(bf16[4,64,512]{2,1,0:T(8,128)(2,1)} %stack.135), calls=%async_computation | async-start | bytes 524288 | tf_op jit(solution)/shard_map/all_to_all | solution.py:35
  97.6 13.7 %collective-permute-start = (f32[7,2,64,128]{3,2,0,1:T(8,128)S(1)}, f32[7,2,64,128]{3,2,0,1:T(8,128)S(1)}, u32[]{:S(2)}, u32[]{:S(2)}) collective-permute-start(f32[7,2,64,128]{3,2,0,1:T(8,128)S(1)} %reduce_sum.9), channel_id=1, source_target_pairs={{0,4},{4,0},{8,12},{12,8},{16,20},{20,16},{24,28},{28,24},{32,36},... | collective-permute-start | bytes 1376264 | tf_op jit(solution)/shard_map/ppermute | solution.py:12
  111.3 12.9 %collective-permute-start.1 = (f32[6,2,64,128]{3,2,0,1:T(8,128)S(1)}, f32[6,2,64,128]{3,2,0,1:T(8,128)S(1)}, u32[]{:S(2)}, u32[]{:S(2)}) collective-permute-start(f32[6,2,64,128]{3,2,0,1:T(8,128)S(1)} %slice_add_fusion), channel_id=1, source_target_pairs={{0,8},{4,12},{8,0},{12,4},{16,24},{20,28},{24,16},{28,20},{32,40},... | collective-permute-start | bytes 1179656 | tf_op jit(solution)/shard_map/ppermute | solution.py:12
  124.3 12.7 %collective-permute-start.2 = (f32[5,2,64,128]{3,2,0,1:T(8,128)S(1)}, f32[5,2,64,128]{3,2,0,1:T(8,128)S(1)}, u32[]{:S(2)}, u32[]{:S(2)}) collective-permute-start(f32[5,2,64,128]{3,2,0,1:T(8,128)S(1)} %slice_add_fusion.1), channel_id=1, source_target_pairs={{0,16},{4,20},{8,24},{12,28},{16,0},{20,4},{24,8},{28,12},{32,48},... | collective-permute-start | bytes 983048 | tf_op jit(solution)/shard_map/ppermute | solution.py:12
  137.0 15.7 %collective-permute-start.3 = (f32[4,2,64,128]{3,2,0,1:T(8,128)S(1)}, f32[4,2,64,128]{3,2,0,1:T(8,128)S(1)}, u32[]{:S(2)}, u32[]{:S(2)}) collective-permute-start(f32[4,2,64,128]{3,2,0,1:T(8,128)S(1)} %slice_add_fusion.2), channel_id=1, source_target_pairs={{0,32},{4,36},{8,40},{12,44},{16,48},{20,52},{24,56},{28,60},{32,0... | collective-permute-start | bytes 786440 | tf_op jit(solution)/shard_map/ppermute | solution.py:12
  152.8 24.2 %collective-permute-start.4 = (f32[3,2,64,128]{3,2,0,1:T(8,128)S(1)}, f32[3,2,64,128]{3,2,0,1:T(8,128)S(1)}, u32[]{:S(2)}, u32[]{:S(2)}) collective-permute-start(f32[3,2,64,128]{3,2,0,1:T(8,128)S(1)} %slice_add_fusion.3), channel_id=1, source_target_pairs={{0,64},{4,68},{8,72},{12,76},{16,80},{20,84},{24,88},{28,92},{32,9... | collective-permute-start | bytes 589832 | tf_op jit(solution)/shard_map/ppermute | solution.py:12
  177.0 6.8 %collective-permute-start.5 = (f32[2,2,64,128]{3,2,0,1:T(8,128)S(1)}, f32[2,2,64,128]{3,2,0,1:T(8,128)S(1)}, u32[]{:S(2)}, u32[]{:S(2)}) collective-permute-start(f32[2,2,64,128]{3,2,0,1:T(8,128)S(1)} %slice_add_fusion.4), channel_id=1, source_target_pairs={{0,128},{4,132},{8,136},{12,140},{16,144},{20,148},{24,152},{28,15... | collective-permute-start | bytes 393224 | tf_op jit(solution)/shard_map/ppermute | solution.py:12
  183.9 7.8 %collective-permute-start.6 = (f32[1,2,64,128]{3,2,0,1:T(8,128)S(1)}, f32[1,2,64,128]{3,2,0,1:T(8,128)S(1)}, u32[]{:S(2)}, u32[]{:S(2)}) collective-permute-start(f32[1,2,64,128]{3,2,0,1:T(8,128)S(1)} %slice_add_fusion.5), channel_id=1, source_target_pairs={{0,256},{4,260},{8,264},{12,268},{16,272},{20,276},{24,280},{28,28... | collective-permute-start | bytes 196616 | tf_op jit(solution)/shard_map/ppermute | solution.py:12
Sparse Core Ops, SparseCore 0:
  17.3 78.5 all-gather.2
